TPU v7x, 512 devices: a whole 4x8x8 slice. The times are simulated.
512 devices in a mesh: hx: 4 (over y_hi), hy: 4 (over x), tok: 32 (over y_lo, z, core).
Axes of the slice: x: 4, y: 8 (y_hi: 4, y_lo: 2; y = y_hi * 2 + y_lo), z: 8, core: 2. Of those that a mesh axis runs over, the one named last changes fastest.
Arguments:
- stream_in: bfloat16 [8192, 4608], P('tok', ('hx', 'hy')), may hold values from -6 to 6
- before_gain: bfloat16 [4608], P(('hx', 'hy')), may hold values from 0.25 to 1.75
- after_gain: bfloat16 [4608], P(('hx', 'hy')), may hold values from 0.25 to 1.75
- feed_gain: bfloat16 [4608], P(('hx', 'hy')), may hold values from 0.25 to 1.75
- query_weight: bfloat16 [4608, 4096], P('tok', ('hx', 'hy')), may hold values from -1 to 1
- key_weight: bfloat16 [4608, 2048], P('tok', ('hx', 'hy')), may hold values from -64 to 64
- value_weight: bfloat16 [4608, 2048], P('tok', ('hx', 'hy')), may hold values from -0.09375 to 0.09375
- output_weight: bfloat16 [4096, 4608], P(('hx', 'hy'), 'tok'), may hold values from -0.09375 to 0.09375
- documents: int32 [8192], P('tok'), may hold values from 0 to 127, never falling along the last dimension, each value on 1 to 128 neighbouring positions
Outputs:
- residual: bfloat16 [8192, 4608], P('tok', ('hx', 'hy'))
- feed_input: bfloat16 [8192, 4608], P('tok', ('hx', 'hy'))
Inputs may be any that keep to these rules, and one draw needn't show every extreme that they name: `documents`: ids never fall along the tokens; a document holds at most 128 tokens and may run across a sequence's end.
All inputs are finite; a program needn't handle non-finite values.
Results may differ from a plain program's by a relative error of at most 0.014.
The roundings to bfloat16 on the way count: a program that leaves them out, or rounds other values in their place, can miss the bound.
Values may be sent and summed in bfloat16 or wider, within the bound.
No kernel may reach another device: no remote copies, remote signals or barrier semaphores. Data moves between devices by JAX's collectives and lax.ppermute only.
A program may use at most 64 MiB of HBM per device.

v0:
```python
import jax
import jax.numpy as jnp
from jax import lax
from jax.sharding import PartitionSpec as P

D = 4608
QH = 32
HEAD = 128
LENGTH = 256
epsilon = 1e-06
neg_big = -1e30


def rows_first(arrays, axis, dims):
    turned = [jnp.moveaxis(a, dim, 0) for a, dim in zip(arrays, dims)]
    both = jnp.concatenate([t.reshape(len(t), -1) for t in turned], axis=1)
    filled, at, finished = (lax.all_gather(both, axis, axis=0, tiled=True), 0, [])
    for t, dim in zip(turned, dims):
        slab = filled[:, at : at + t[0].size].reshape(-1, *t.shape[1:])
        finished.append(jnp.moveaxis(slab, 0, dim))
        at += t[0].size
    return tuple(finished)


def side_by_side(arrays, axis, dim, along):
    widths = [a.shape[along] for a in arrays]
    both = jnp.concatenate(arrays, axis=along)
    filled = lax.all_gather(both, axis, axis=dim, tiled=True)
    return tuple(jnp.split(filled, [sum(widths[:k]) for k in range(1, len(widths))], axis=along))


def copy_for_each(value, axis):
    copies = jnp.broadcast_to(value, (lax.axis_size(axis), *value.shape))
    return lax.all_to_all(copies, axis, split_axis=0, concat_axis=0, tiled=True)


def joined_along(parts, dim):
    dims = list(parts.shape[1:])
    dims[dim] *= parts.shape[0]
    return jnp.moveaxis(parts, 0, dim).reshape(dims)


def gathered_copies(value, axis, dim):
    parts = copy_for_each(value, axis)
    return joined_along(parts, dim)


def over_copies(value, axis):
    return copy_for_each(value, axis).sum(axis=0)


def in_one(arrays, axis):
    ravelled, at, finished = (jnp.concatenate([a.reshape(-1) for a in arrays]), 0, [])
    subtotal = over_copies(ravelled, axis)
    for a in arrays:
        finished.append(subtotal[at : at + a.size].reshape(a.shape))
        at += a.size
    return tuple(finished)


def rotate(values, positions):
    half_width = values.shape[-1] // 2
    frequency = 10000.0 ** (-jnp.arange(half_width, dtype=jnp.float32) / half_width)
    angles = positions.astype(jnp.float32)[:, None] * frequency[None, :]
    cosine_table = jnp.cos(angles)[:, None, :]
    sine_table = jnp.sin(angles)[:, None, :]
    leading = values[..., :half_width]
    trailing = values[..., half_width:]
    return jnp.concatenate(
        [
            leading * cosine_table - trailing * sine_table,
            trailing * cosine_table + leading * sine_table,
        ],
        axis=-1,
    )


def per_device(
    stream_in,
    before_gain,
    after_gain,
    feed_gain,
    query_weight,
    key_weight,
    value_weight,
    output_weight,
    documents,
):
    rows = stream_in.shape[0]
    wide = stream_in.astype(jnp.float32)
    raw_rows, gain_whole = rows_first((stream_in, before_gain), ("hx", "hy"), (1, 0))
    raw_wide = raw_rows.astype(jnp.float32)
    first_sq = jnp.sum(raw_wide * raw_wide, axis=1)
    first_scale = lax.rsqrt(first_sq / D + epsilon)
    normed = (raw_wide * first_scale[:, None] * gain_whole.astype(jnp.float32)[None, :]).astype(
        jnp.bfloat16
    )
    pieces = side_by_side((query_weight, key_weight, value_weight), "tok", 0, 1)
    query_sum, key_sum, value_sum = tuple(
        (jnp.dot(normed, piece, preferred_element_type=jnp.float32) for piece in pieces)
    )
    query_heads = query_weight.shape[1] // HEAD
    key_heads = key_weight.shape[1] // HEAD
    ratio = query_heads // key_heads
    positions = jnp.arange(rows, dtype=jnp.int32) % LENGTH
    count_seq = rows // LENGTH
    queries = (
        (rotate(query_sum.reshape(rows, query_heads, HEAD), positions) * (D / QH) ** (-0.5))
        .astype(jnp.bfloat16)
        .reshape(count_seq, LENGTH, key_heads, ratio, HEAD)
    )
    keys = (
        rotate(key_sum.reshape(rows, key_heads, HEAD), positions)
        .astype(jnp.bfloat16)
        .reshape(count_seq, LENGTH, key_heads, HEAD)
    )
    values = value_sum.astype(jnp.bfloat16).reshape(count_seq, LENGTH, key_heads, HEAD)
    doc_seq = documents.reshape(count_seq, LENGTH)

    def one_sequence(items):
        query_part, key_part, value_part, doc_part = items
        scores = jnp.einsum(
            "tkrh,skh->tkrs", query_part, key_part, preferred_element_type=jnp.float32
        )
        index = jnp.arange(LENGTH)
        allowed = (index[None, :] <= index[:, None]) & (doc_part[None, :] == doc_part[:, None])
        mask = allowed[:, None, None, :]
        best = jnp.max(jnp.where(mask, scores, neg_big), axis=-1, keepdims=True)
        weights = jnp.where(mask, jnp.exp(scores - best), 0.0)
        total = jnp.sum(weights, axis=-1)
        summed = jnp.einsum(
            "tkrs,skh->tkrh",
            weights.astype(jnp.bfloat16),
            value_part,
            preferred_element_type=jnp.float32,
        )
        return (summed / total[..., None]).astype(jnp.bfloat16)

    attended = lax.map(one_sequence, (queries, keys, values, doc_seq)).reshape(
        rows, query_heads * HEAD
    )
    terms = jnp.dot(
        attended, gathered_copies(output_weight, "tok", 1), preferred_element_type=jnp.float32
    )
    mixed = lax.psum_scatter(
        terms.astype(jnp.bfloat16), ("hx", "hy"), scatter_dimension=1, tiled=True
    ).astype(jnp.float32)
    gain_after = after_gain.astype(jnp.float32)[None, :]
    gain_feed = feed_gain.astype(jnp.float32)[None, :]
    branch = mixed * gain_after
    after_sq, cross_sum, branch_sq = in_one(
        (
            jnp.sum(mixed * mixed, axis=1),
            jnp.sum(wide * branch, axis=1),
            jnp.sum(branch * branch, axis=1),
        ),
        ("hx", "hy"),
    )
    after_scale = lax.rsqrt(after_sq / D + epsilon)
    residual = (wide + mixed * after_scale[:, None] * gain_after).astype(jnp.bfloat16)
    residual_wide = residual.astype(jnp.float32)
    feed_sq = first_sq + 2.0 * after_scale * cross_sum + after_scale * after_scale * branch_sq
    feed_scale = lax.rsqrt(feed_sq / D + epsilon)
    feed_input = (residual_wide * feed_scale[:, None] * gain_feed).astype(jnp.bfloat16)
    return (residual, feed_input)


def solution(mesh):
    in_specs = (
        P("tok", ("hx", "hy")),
        P(("hx", "hy")),
        P(("hx", "hy")),
        P(("hx", "hy")),
        P("tok", ("hx", "hy")),
        P("tok", ("hx", "hy")),
        P("tok", ("hx", "hy")),
        P(("hx", "hy"), "tok"),
        P("tok"),
    )
    out_specs = (P("tok", ("hx", "hy")), P("tok", ("hx", "hy")))
    return jax.shard_map(
        per_device, mesh=mesh, in_specs=in_specs, out_specs=out_specs, check_vma=False
    )
```

profile of v0, /device:TPU:8, one launch (start us, length us, event | category | flops | bytes accessed | tf_op | source)
XLA Modules:
  0.0 299.1 jit_solution(16729745893624223635)
XLA Ops:
  7.2 1.1 copy.42
  8.3 0.7 reshape.243
  9.0 0.7 maximum_bitcast_fusion
  9.7 0.0 all-gather.4.cloned.1.call-start
  9.7 1.6 pad_maximum_fusion
  11.4 2.5 broadcast_in_dim.63
  13.8 12.1 %all-to-all-start = ((bf16[32,256,144]{1,2,0:T(8,128)(2,1)}), bf16[32,256,144]{1,2,0:T(8,128)(2,1)S(1)}, u32[]{:S(2)}, u32[]{:S(2)}) async-start(bf16[32,256,144]{1,2,0:T(8,128)(2,1)} %broadcast_in_dim.63), calls=%async_computation | async-start | bytes 4718592 | tf_op jit(solution)/shard_map/all_to_all | solution.py:34
  25.9 0.0 reduce-scatter.2.cloned.1.call-start
  26.0 0.1 fusion.35
  26.1 0.5 multiply_cosine_fusion
  26.6 66.1 %all-gather.6.cloned.1.call-done = bf16[16,288,257]{1,2,0:T(8,128)(2,1)} async-done(((bf16[1,288,257]{1,2,0:T(8,128)(2,1)}), bf16[16,288,257]{1,2,0:T(8,128)(2,1)}) %all-gather.6.cloned.1.call-update) | async-done | bytes 2368528 | tf_op jit(solution)/shard_map/all_gather | solution.py:17
  92.7 4.1 %copy.43 = bf16[16,288,257]{1,0,2:T(8,128)(2,1)} copy(bf16[16,288,257]{1,2,0:T(8,128)(2,1)} %all-gather.6.cloned.1.call-done) | data formatting | bytes 4737024 | tf_op jit(solution)/shard_map/all_gather | solution.py:17
  96.8 6.2 %reshape.251 = bf16[4608,257]{0,1:T(8,128)(2,1)} reshape(bf16[16,288,257]{1,0,2:T(8,128)(2,1)} %copy.43) | data formatting | bytes 4737024
  103.0 0.9 fusion.51
  103.9 2.2 fusion
  106.2 58.8 %all-gather.4.cloned.1.call-done = bf16[4608,512]{1,0:T(8,128)(2,1)} async-done(((bf16[144,512]{1,0:T(8,128)(2,1)}), bf16[4608,512]{1,0:T(8,128)(2,1)}) %all-gather.4.cloned.1.call-update) | async-done | bytes 4718608 | tf_op jit(solution)/shard_map/all_gather | solution.py:28
  164.9 3.6 %fusion.3 = f32[256,256]{0,1:T(8,128)S(1)} fusion(bf16[4608,512]{1,0:T(8,128)(2,1)} %all-gather.4.cloned.1.call-done, f32[4608]{0:T(1024)S(1)} %fusion.51, f32[256]{0:T(256)S(1)} %add_rsqrt_fusion.2, bf16[4608,257]{0,1:T(8,128)(2,1)} %reshape.251), kind=kOutput, calls=%fused_computation.6 | convolution fusion | flops 608698368 | bytes 5000192 | tf_op jit(solution)/shard_map/dot_general | solution.py:100
  168.6 0.1 copy.56
  168.7 0.1 copy.57
  168.9 3.0 %fusion.9 = f32[256,1,128]{0,2,1:T(8,128)S(1)} fusion(bf16[4608,512]{1,0:T(8,128)(2,1)} %all-gather.4.cloned.1.call-done, f32[4608]{0:T(1024)S(1)} %fusion.51, f32[256]{0:T(256)S(1)} %add_rsqrt_fusion.2, bf16[4608,257]{0,1:T(8,128)(2,1)} %reshape.251), kind=kOutput, calls=%fused_computation.14 | convolution fusion | flops 306708480 | bytes 3689472 | tf_op jit(solution)/shard_map/dot_general | solution.py:100
  171.9 0.3 fusion.50
  172.2 0.1 multiply_subtract_fusion
  172.3 0.4 select_reduce_fusion
  172.7 0.1 fusion.22
  172.8 3.1 %fusion.19 = bf16[1,128,256,2]{2,1,3,0:T(8,128)(2,1)S(1)} fusion(bf16[4608,512]{1,0:T(8,128)(2,1)} %all-gather.4.cloned.1.call-done, f32[256,1,2,256]{0,3,2,1:T(8,128)S(1)} %get-tuple-element.36, f32[256,2]{0,1:T(2,128)S(1)} %get-tuple-element.35, pred[256,256]{0,1:T(8,128)(4,1)S(1)} %fusion.35, f32[256,2]{0,1:T(2,128)S(1)} %fusion.22, ...), kind=kOutput, calls=%fused_computation.18 | convolution fusion | flops 340819968 | bytes 4283392 | tf_op jit(solution)/shard_map/while/body/eval_jaxpr/tkrs,skh->tkrh/dot_general | solution.py:131
  175.9 2.2 convolution_convert_fusion
  178.1 94.7 %reduce-scatter.2.cloned.1.call-done = bf16[256,288]{0,1:T(8,128)(2,1)} async-done(((bf16[256,4608]{0,1:T(8,128)(2,1)}), bf16[256,288]{0,1:T(8,128)(2,1)}) %reduce-scatter.2.cloned.1.call-update) | async-done | bytes 147472 | tf_op jit(solution)/shard_map/reduce_scatter | solution.py:145
  272.8 1.0 fusion.26
  273.9 0.6 broadcast_in_dim.64
  274.5 6.3 %all-to-all-start.1 = ((f32[16,1,768]{2,1,0:T(1,128)}), f32[16,1,768]{2,1,0:T(1,128)S(1)}, u32[]{:S(2)}, u32[]{:S(2)}) async-start(f32[16,1,768]{2,1,0:T(1,128)} %broadcast_in_dim.64), calls=%async_computation.2 | async-start | bytes 98304 | tf_op jit(solution)/shard_map/all_to_all | solution.py:34
  280.8 10.0 %all-to-all-done.1 = f32[16,1,768]{2,1,0:T(1,128)S(1)} async-done(((f32[16,1,768]{2,1,0:T(1,128)}), f32[16,1,768]{2,1,0:T(1,128)S(1)}, u32[]{:S(2)}, u32[]{:S(2)}) %all-to-all-start.1) | async-done | bytes 49184 | tf_op jit(solution)/shard_map/all_to_all | solution.py:34
  290.9 1.8 multiply_convert_fusion
  (22 shorter events, 0.2 us)
Async XLA Ops:
  7.2 85.5 %all-gather.6.cloned.1.call-start = ((), (), s32[]{:S(2)}) async-start(), calls=%async_computation.5 | async-start | bytes 3446784 | tf_op jit(solution)/shard_map/all_gather | solution.py:17
  9.7 155.2 %all-gather.4.cloned.1.call-start = ((), (), s32[]{:S(2)}) async-start(), calls=%async_computation.3 | async-start | bytes 4866048 | tf_op jit(solution)/shard_map/all_gather | solution.py:28
  13.8 12.2 %copy-start.1 = (s32[256]{0:T(256)S(1)}, s32[256]{0:T(256)}, u32[]{:S(2)}) copy-start(s32[256]{0:T(256)} %param.17) | copy-start | bytes 3076
  13.8 162.0 %all-to-all-start = ((bf16[32,256,144]{1,2,0:T(8,128)(2,1)}), bf16[32,256,144]{1,2,0:T(8,128)(2,1)S(1)}, u32[]{:S(2)}, u32[]{:S(2)}) async-start(bf16[32,256,144]{1,2,0:T(8,128)(2,1)} %broadcast_in_dim.63), calls=%async_computation | async-start | bytes 4718592 | tf_op jit(solution)/shard_map/all_to_all | solution.py:34
  25.9 246.9 %reduce-scatter.2.cloned.1.call-start = ((), (), s32[]{:S(2)}) async-start(), calls=%async_computation.4 | async-start | bytes 2506752 | tf_op jit(solution)/shard_map/reduce_scatter | solution.py:145
  175.9 2.2 copy-start.2
  178.1 94.7 %copy-start = (bf16[256,288]{0,1:T(8,128)(2,1)S(1)}, bf16[256,288]{0,1:T(8,128)(2,1)}, u32[]{:S(2)}) copy-start(bf16[256,288]{0,1:T(8,128)(2,1)} %param.9) | copy-start | bytes 442372
  178.1 102.7 %copy-start.3 = (bf16[288]{0:T(512)(128)(2,1)S(1)}, bf16[288]{0:T(512)(128)(2,1)}, u32[]{:S(2)}) copy-start(bf16[288]{0:T(512)(128)(2,1)} %param.12) | copy-start | bytes 1732
  274.5 16.3 %all-to-all-start.1 = ((f32[16,1,768]{2,1,0:T(1,128)}), f32[16,1,768]{2,1,0:T(1,128)S(1)}, u32[]{:S(2)}, u32[]{:S(2)}) async-start(f32[16,1,768]{2,1,0:T(1,128)} %broadcast_in_dim.64), calls=%async_computation.2 | async-start | bytes 98304 | tf_op jit(solution)/shard_map/all_to_all | solution.py:34
Sparse Core Ops, SparseCore 0:
  11.0 81.6 all-gather.5
  95.4 69.4 all-gather.3
  178.2 94.5 reduce-scatter.1
where the time goes:
time: 300 us; the launch traced here: 299 us
  waiting for transfers between devices  230 us (77%)
  starting transfers between devices  18.5 us (6%)
  local copies, waits for them, and re-layouts  15.5 us (5%)
  between operations  13.9 us (5%)
  matrix products  12.3 us (4%)
  other arithmetic  9.49 us (3%)
    reduce_scatter x1, waiting for transfers between devices, per_device(): lax.psum_scatter(terms.astype(jnp.bfloat16), ('hx', 'hy'), scatter_dimens...  94.7 us
    all_gather x1, waiting for transfers between devices, rows_first(): lax.all_gather(both, axis, axis=0, tiled=True)  66.1 us
    all_gather x1, waiting for transfers between devices, side_by_side(): filled = lax.all_gather(both, axis, axis=dim, tiled=True)  58.8 us
    all_to_all x2, starting transfers between devices, copy_for_each(): return lax.all_to_all(copies, axis, split_axis=0, concat_axis=0, tiled=True)  18.3 us
    all_to_all x2, waiting for transfers between devices, copy_for_each(): return lax.all_to_all(copies, axis, split_axis=0, concat_axis=0, tiled=True)  10 us
    unnamed x12, local copies, waits for them, and re-layouts  7.58 us
    dot_general x2, matrix products, per_device(): jnp.dot(normed, piece, preferred_element_type=jnp.float32)  6.66 us
  transfers between devices with their start and end apart: 5, of which 4 were waited for; matrix products, arithmetic and copies ran while one was open for 10% of the time, Pallas kernels for 0%

commit v1 on v0

--- a/solution.py
+++ b/solution.py
@@ -14,7 +14,13 @@
 def rows_first(arrays, axis, dims):
     turned = [jnp.moveaxis(a, dim, 0) for a, dim in zip(arrays, dims)]
     both = jnp.concatenate([t.reshape(len(t), -1) for t in turned], axis=1)
-    filled, at, finished = (lax.all_gather(both, axis, axis=0, tiled=True), 0, [])
+    filled, at, finished = (
+        jnp.concatenate(
+            lax.all_to_all(jnp.stack([both] * lax.axis_size(axis)), axis, 0, 0), axis=0
+        ),
+        0,
+        [],
+    )
     for t, dim in zip(turned, dims):
         slab = filled[:, at : at + t[0].size].reshape(-1, *t.shape[1:])
         finished.append(jnp.moveaxis(slab, 0, dim))

time: 300 us -> 310 us (1.033)
  blocking collectives: 0 us -> 110 us
  waiting for transfers between devices: 230 us -> 130 us
    all_to_all x0 -> x1, blocking collectives: none -> 110 us  [rows_first(): lax.all_to_all(jnp.stack([both] * lax.axis_size(axis)), axis, 0, 0)]
    all_gather x1 -> x0, waiting for transfers between devices: 66.1 us -> none  [rows_first(): lax.all_gather(both, axis, axis=0, tiled=True)]
    all_gather x1, waiting for transfers between devices: 58.8 us -> 0.02 us  [side_by_side(): filled = lax.all_gather(both, axis, axis=dim, tiled=True)]
    all_to_all x2, waiting for transfers between devices: 10 us -> 39.9 us  [copy_for_each(): return lax.all_to_all(copies, axis, split_axis=0, concat_axis=0, tiled=True)]
    unnamed x12, local copies, waits for them, and re-layouts: 7.58 us -> 0.27 us
    reshape x0 -> x1, local copies, waits for them, and re-layouts: none -> 6.24 us  [rows_first(): jnp.concatenate(lax.all_to_all(jnp.stack([both] * lax.axis_size(axis)), a...]
    reduce_scatter x1, waiting for transfers between devices: 94.7 us -> 90.6 us  [per_device(): lax.psum_scatter(terms.astype(jnp.bfloat16), ('hx', 'hy'), scatter_dimens...]
    all_to_all x0 -> x1, local copies, waits for them, and re-layouts: none -> 4.07 us  [rows_first(): lax.all_to_all(jnp.stack([both] * lax.axis_size(axis)), axis, 0, 0)]
  transfers between devices with their start and end apart: 5 -> 4, of which waited for: 4 -> 3; matrix products, arithmetic and copies ran while one was open for 10% -> 9% of each run, Pallas kernels for 0% -> 0%
where the time goes in v1:
time: 310 us; the launch traced here: 309 us
  waiting for transfers between devices  130 us (42%)
  blocking collectives  110 us (35%)
  starting transfers between devices  18.4 us (6%)
  between operations  14.2 us (5%)
  local copies, waits for them, and re-layouts  14.1 us (5%)
  matrix products  12.3 us (4%)
  other arithmetic  9.73 us (3%)
    all_to_all x1, blocking collectives, rows_first(): lax.all_to_all(jnp.stack([both] * lax.axis_size(axis)), axis, 0, 0)  110 us
    reduce_scatter x1, waiting for transfers between devices, per_device(): lax.psum_scatter(terms.astype(jnp.bfloat16), ('hx', 'hy'), scatter_dimens...  90.6 us
    all_to_all x2, waiting for transfers between devices, copy_for_each(): return lax.all_to_all(copies, axis, split_axis=0, concat_axis=0, tiled=True)  39.9 us
    all_to_all x2, starting transfers between devices, copy_for_each(): return lax.all_to_all(copies, axis, split_axis=0, concat_axis=0, tiled=True)  18.4 us
    dot_general x2, matrix products, per_device(): jnp.dot(normed, piece, preferred_element_type=jnp.float32)  6.66 us
    reshape x1, local copies, waits for them, and re-layouts, rows_first(): jnp.concatenate(lax.all_to_all(jnp.stack([both] * lax.axis_size(axis)), a...  6.24 us
  transfers between devices with their start and end apart: 4, of which 3 were waited for; matrix products, arithmetic and copies ran while one was open for 9% of the time, Pallas kernels for 0%

profile of v1, /device:TPU:8, one launch (start us, length us, event | category | flops | bytes accessed | tf_op | source)
XLA Modules:
  0.0 309.2 jit_solution(14369749622249803509)
XLA Ops:
  7.2 1.6 pad_maximum_fusion.1
  8.8 0.8 reshape.258
  9.6 0.9 pad_maximum_fusion
  10.6 0.2 copy.46
  10.7 0.3 stack.2
  11.0 110.0 %all_to_all.16 = bf16[16,288,257]{1,2,0:T(8,128)(2,1)} all-to-all(bf16[16,288,257]{1,2,0:T(8,128)(2,1)S(1)} %stack.2), channel_id=1, replica_groups=mesh['hx'=4,'hy'=4,'tok'=32] {'hx','hy'}, dimensions={0} | all-to-all | bytes 4737024 | tf_op jit(solution)/shard_map/all_to_all | solution.py:19
  121.0 1.6 broadcast_in_dim.63
  122.6 12.1 %all-to-all-start.1 = ((bf16[32,256,144]{1,2,0:T(8,128)(2,1)}), bf16[32,256,144]{1,2,0:T(8,128)(2,1)S(1)}, u32[]{:S(2)}, u32[]{:S(2)}) async-start(bf16[32,256,144]{1,2,0:T(8,128)(2,1)} %broadcast_in_dim.63), calls=%async_computation.1 | async-start | bytes 4718592 | tf_op jit(solution)/shard_map/all_to_all | solution.py:40
  134.7 0.0 reduce-scatter.2.cloned.1.call-start
  134.8 0.1 fusion.35
  134.9 0.5 multiply_cosine_fusion
  135.4 4.1 %copy.47 = bf16[16,288,257]{1,0,2:T(8,128)(2,1)} copy(bf16[16,288,257]{1,2,0:T(8,128)(2,1)} %all_to_all.16) | data formatting | bytes 4737024 | tf_op jit(solution)/shard_map/all_to_all | solution.py:19
  139.5 6.2 %reshape.249 = bf16[4608,257]{0,1:T(8,128)(2,1)} reshape(bf16[16,288,257]{1,0,2:T(8,128)(2,1)} %copy.47) | data formatting | bytes 4737024 | tf_op jit(solution)/shard_map/reshape | solution.py:18
  145.7 0.9 fusion.51
  146.7 2.2 fusion
  148.9 3.6 %fusion.3 = f32[256,256]{0,1:T(8,128)S(1)} fusion(bf16[4608,512]{1,0:T(8,128)(2,1)} %all-gather.2.cloned.1.call-done, f32[4608]{0:T(1024)S(1)} %fusion.51, f32[256]{0:T(256)S(1)} %add_rsqrt_fusion.2, bf16[4608,257]{0,1:T(8,128)(2,1)} %reshape.249), kind=kOutput, calls=%fused_computation.6 | convolution fusion | flops 608698368 | bytes 5000192 | tf_op jit(solution)/shard_map/dot_general | solution.py:106
  152.6 0.1 copy.60
  152.7 0.1 copy.61
  152.8 3.0 fusion.9
  155.9 0.3 fusion.50
  156.2 0.1 multiply_subtract_fusion
  156.3 0.4 select_reduce_fusion
  156.6 0.1 fusion.22
  156.8 3.1 fusion.19
  159.8 29.9 %all-to-all-done.1 = bf16[32,256,144]{1,2,0:T(8,128)(2,1)S(1)} async-done(((bf16[32,256,144]{1,2,0:T(8,128)(2,1)}), bf16[32,256,144]{1,2,0:T(8,128)(2,1)S(1)}, u32[]{:S(2)}, u32[]{:S(2)}) %all-to-all-start.1) | async-done | bytes 2359328 | tf_op jit(solution)/shard_map/all_to_all | solution.py:40
  189.7 2.2 convolution_convert_fusion
  191.9 90.6 %reduce-scatter.2.cloned.1.call-done = bf16[256,288]{0,1:T(8,128)(2,1)} async-done(((bf16[256,4608]{0,1:T(8,128)(2,1)}), bf16[256,288]{0,1:T(8,128)(2,1)}) %reduce-scatter.2.cloned.1.call-update) | async-done | bytes 147472 | tf_op jit(solution)/shard_map/reduce_scatter | solution.py:151
  282.5 1.0 fusion.26
  283.6 0.6 broadcast_in_dim.64
  284.2 6.3 %all-to-all-start.2 = ((f32[16,1,768]{2,1,0:T(1,128)}), f32[16,1,768]{2,1,0:T(1,128)S(1)}, u32[]{:S(2)}, u32[]{:S(2)}) async-start(f32[16,1,768]{2,1,0:T(1,128)} %broadcast_in_dim.64), calls=%async_computation.3 | async-start | bytes 98304 | tf_op jit(solution)/shard_map/all_to_all | solution.py:40
  290.5 10.0 %all-to-all-done.2 = f32[16,1,768]{2,1,0:T(1,128)S(1)} async-done(((f32[16,1,768]{2,1,0:T(1,128)}), f32[16,1,768]{2,1,0:T(1,128)S(1)}, u32[]{:S(2)}, u32[]{:S(2)}) %all-to-all-start.2) | async-done | bytes 49184 | tf_op jit(solution)/shard_map/all_to_all | solution.py:40
  300.6 1.8 multiply_convert_fusion
  (23 shorter events, 0.2 us)
Async XLA Ops:
  7.2 141.7 %all-gather.2.cloned.1.call-start = ((), (), s32[]{:S(2)}) async-start(), calls=%async_computation.4 | async-start | bytes 4866048 | tf_op jit(solution)/shard_map/all_gather | solution.py:34
  11.0 110.0 %copy-start.1 = (bf16[256,144]{0,1:T(8,128)(2,1)S(1)}, bf16[256,144]{0,1:T(8,128)(2,1)}, u32[]{:S(2)}) copy-start(bf16[256,144]{0,1:T(8,128)(2,1)} %param.16) | copy-start | bytes 221188
  122.6 12.2 %copy-start.2 = (s32[256]{0:T(256)S(1)}, s32[256]{0:T(256)}, u32[]{:S(2)}) copy-start(s32[256]{0:T(256)} %param.17) | copy-start | bytes 3076
  122.6 67.1 %all-to-all-start.1 = ((bf16[32,256,144]{1,2,0:T(8,128)(2,1)}), bf16[32,256,144]{1,2,0:T(8,128)(2,1)S(1)}, u32[]{:S(2)}, u32[]{:S(2)}) async-start(bf16[32,256,144]{1,2,0:T(8,128)(2,1)} %broadcast_in_dim.63), calls=%async_computation.1 | async-start | bytes 4718592 | tf_op jit(solution)/shard_map/all_to_all | solution.py:40
  134.7 147.8 %reduce-scatter.2.cloned.1.call-start = ((), (), s32[]{:S(2)}) async-start(), calls=%async_computation.5 | async-start | bytes 2506752 | tf_op jit(solution)/shard_map/reduce_scatter | solution.py:151
  189.7 2.2 copy-start.3
  191.9 90.6 %copy-start = (bf16[256,288]{0,1:T(8,128)(2,1)S(1)}, bf16[256,288]{0,1:T(8,128)(2,1)}, u32[]{:S(2)}) copy-start(bf16[256,288]{0,1:T(8,128)(2,1)} %param.9) | copy-start | bytes 442372
  191.9 98.6 %copy-start.4 = (bf16[288]{0:T(512)(128)(2,1)S(1)}, bf16[288]{0:T(512)(128)(2,1)}, u32[]{:S(2)}) copy-start(bf16[288]{0:T(512)(128)(2,1)} %param.12) | copy-start | bytes 1732
  284.2 16.3 %all-to-all-start.2 = ((f32[16,1,768]{2,1,0:T(1,128)}), f32[16,1,768]{2,1,0:T(1,128)S(1)}, u32[]{:S(2)}, u32[]{:S(2)}) async-start(f32[16,1,768]{2,1,0:T(1,128)} %broadcast_in_dim.64), calls=%async_computation.3 | async-start | bytes 98304 | tf_op jit(solution)/shard_map/all_to_all | solution.py:40
Sparse Core Ops, SparseCore 0:
  10.7 97.2 all-gather.1
  192.0 90.4 reduce-scatter.1
